TPU v7x, 32 devices: a whole 2x2x4 slice. The times are simulated.
32 devices in a mesh: grp: 4 (over z), cand: 8 (over y, x, core).
Axes of the slice: x: 2, y: 2, z: 4, core: 2. Of those that a mesh axis runs over, the one named last changes fastest.
Arguments:
- embeddings: bfloat16 [96, 1024, 1024], P('grp', 'cand'), may hold values from -6 to 6
- hidden_weight: bfloat16 [2048, 1024], P('cand'), may hold values from -0.1875 to 0.1875
- score_weight: bfloat16 [2048], replicated, may hold values from -0.5 to 0.5
- relevance: int32 [96, 1024], P('grp', 'cand'), may hold values from 0 to 4
- rank_pos: int32 [96, 1024], P('grp', 'cand'), may hold values from 0 to 1023, as said below
- ideal_dcg: float32 [96], P('grp'), may hold values from 32 to 128
Outputs:
- grad_hidden: float32 [2048, 1024], P('cand')
- lambdas: float32 [96, 1024], P('grp', 'cand')
Inputs may be any that keep to these rules, and one draw needn't show every extreme that they name: `rank_pos`: in each group the rank positions are a permutation of 0 to 1023.
All inputs are finite; a program needn't handle non-finite values.
Results may differ from a plain program's by a relative error of at most 0.006.
Values may be sent and summed in bfloat16 or wider, within the bound.
A program may use at most 64 MiB of HBM per device.

v0:
```python
import jax
import jax.numpy as jnp
from jax import lax
from jax.sharding import PartitionSpec as P

EPS = 1e-06


def pair_lambdas(own_score, own_gain, own_disc, far_score, far_gain, far_disc, ideal):
    gain_diff = far_gain[..., None, :] - own_gain[..., :, None]
    toward = jnp.sign(gain_diff)
    weight = (
        jnp.abs(gain_diff)
        * jnp.abs(far_disc[..., None, :] - own_disc[..., :, None])
        / ideal[..., None, None]
    )
    margin = own_score[..., :, None] - far_score[..., None, :]
    return jnp.sum(weight * toward * jax.nn.sigmoid(toward * margin), axis=-1)


def gain_of(labels):
    return jnp.exp2(labels.astype(jnp.float32)) - 1.0


def discount_of(positions):
    return 1.0 / jnp.log2(2.0 + positions.astype(jnp.float32))


def per_device(embeddings, hidden_weight, score_weight, relevance, rank_pos, ideal_dcg):
    grp_count, local, width = embeddings.shape
    cand_rows = embeddings.reshape(grp_count * local, width)
    pre_act = lax.dot_general(
        cand_rows,
        lax.all_gather(hidden_weight, "cand", axis=0, tiled=True),
        (((1,), (1,)), ((), ())),
        preferred_element_type=jnp.float32,
    )
    acts, pull = jax.vjp(jax.nn.gelu, pre_act)
    scores = jnp.dot(
        acts.astype(jnp.bfloat16), score_weight, preferred_element_type=jnp.float32
    ).reshape(grp_count, local)
    gain_vals = gain_of(relevance)
    discount = discount_of(rank_pos)
    lambdas = pair_lambdas(
        scores,
        gain_vals,
        discount,
        lax.all_gather(scores, "cand", axis=1, tiled=True),
        lax.all_gather(gain_vals, "cand", axis=1, tiled=True),
        lax.all_gather(discount, "cand", axis=1, tiled=True),
        ideal_dcg,
    )
    upstream = (
        lambdas.reshape(grp_count * local)[:, None] * score_weight.astype(jnp.float32)[None, :]
    )
    grad_pre = pull(upstream)[0].astype(jnp.bfloat16)
    owned = lax.psum_scatter(
        lax.dot_general(
            grad_pre, cand_rows, (((0,), (0,)), ((), ())), preferred_element_type=jnp.float32
        ).astype(jnp.bfloat16),
        "cand",
        scatter_dimension=0,
        tiled=True,
    ).astype(jnp.float32)
    summed = lax.psum(owned, "grp")
    squares = lax.psum(jnp.sum(summed * summed), "cand")
    entries = summed.shape[0] * summed.shape[1] * lax.axis_size("cand")
    scale = lax.rsqrt(squares / entries + EPS)
    return (summed * scale, lambdas)


def solution(mesh):
    return jax.shard_map(
        per_device,
        mesh=mesh,
        in_specs=(
            P("grp", "cand", None),
            P("cand", None),
            P(),
            P("grp", "cand"),
            P("grp", "cand"),
            P("grp"),
        ),
        out_specs=(P("cand", None), P("grp", "cand")),
        check_vma=False,
    )
```

profile of v0, /device:TPU:0, one launch (start us, length us, event | category | flops | bytes accessed | tf_op | source)
XLA Modules:
  0.0 254.7 jit_solution(1957202030902142692)
XLA Ops:
  7.2 0.0 all-gather.2.cloned.1.call-start
  7.2 0.7 all-gather.2.cloned.1.call-update
  7.9 0.0 reduce-scatter.2.cloned.1.call-start
  7.9 0.7 reshape.18
  8.6 0.7 convert_element_type.24
  9.3 0.7 exponential_add_fusion
  10.0 10.7 %all_gather.12 = f32[24,1024]{1,0:T(8,128)S(1)} all-gather(f32[24,128]{1,0:T(8,128)S(1)} %exponential_add_fusion), channel_id=1, replica_groups=mesh['grp'=4,'cand'=8] {'cand'}, dimensions={1}, use_global_device_ids=true | all-gather | bytes 110592 | tf_op jit(solution)/shard_map/all_gather | solution.py:49
  20.7 0.7 multiply_divide_fusion
  21.5 9.5 %all_gather.13 = f32[24,1024]{1,0:T(8,128)S(1)} all-gather(f32[24,128]{1,0:T(8,128)S(1)} %multiply_divide_fusion), channel_id=1, replica_groups=mesh['grp'=4,'cand'=8] {'cand'}, dimensions={1}, use_global_device_ids=true | all-gather | bytes 110592 | tf_op jit(solution)/shard_map/all_gather | solution.py:50
  31.0 18.5 %all-gather.2.cloned.1.call-done = bf16[2048,1024]{1,0:T(8,128)(2,1)} async-done(((bf16[256,1024]{1,0:T(8,128)(2,1)}), bf16[2048,1024]{1,0:T(8,128)(2,1)}) %all-gather.2.cloned.1.call-update) | async-done | bytes 4194320 | tf_op jit(solution)/shard_map/all_gather | solution.py:34
  49.5 19.7 %fusion.36 = f32[3072,2048]{1,0:T(8,128)} fusion(bf16[3072,1024]{1,0:T(8,128)(2,1)} %bitcast.11, bf16[2048,1024]{1,0:T(8,128)(2,1)} %all-gather.2.cloned.1.call-done), kind=kOutput, calls=%fused_computation.44 | convolution fusion | flops 12884901888 | bytes 35651584 | tf_op jit(solution)/shard_map/dot_general | solution.py:32
  69.1 0.0 copy-start
  69.1 11.9 %fusion.20 = f32[1,3072]{1,0:T(1,128)S(1)} fusion(bf16[2048,1]{0,1:T(2,128)(2,1)S(1)} %reshape.18, f32[3072,2048]{1,0:T(8,128)} %fusion.36), kind=kOutput, calls=%fused_computation.27 | convolution fusion | flops 69206016 | bytes 25182208 | tf_op jit(solution)/shard_map/dot_general | solution.py:39
  81.1 9.1 %all_gather.15 = f32[24,1024]{1,0:T(8,128)S(1)} all-gather(f32[24,128]{1,0:T(8,128)S(1)} %bitcast.9), channel_id=1, replica_groups=mesh['grp'=4,'cand'=8] {'cand'}, dimensions={1}, use_global_device_ids=true | all-gather | bytes 110592 | tf_op jit(solution)/shard_map/all_gather | solution.py:48
  90.2 0.0 copy-done
  90.2 11.2 %fusion.13 = f32[24,128]{1,0:T(8,128)S(1)} fusion(f32[24,1024]{1,0:T(8,128)S(1)} %all_gather.15, f32[24,128]{1,0:T(8,128)S(1)} %bitcast.10, f32[24]{0:T(128)S(1)} %copy-done, f32[24,128]{1,0:T(8,128)S(1)} %multiply_divide_fusion, f32[24,1024]{1,0:T(8,128)S(1)} %all_gather.13, f32[24,128]{1,0:T(8,128)S(1)} %exponential_add_fusion, f32[24,1024]{1,0:T(8,128)S(1)} %all_gather.12), kind=kLoop, calls=%fused_computation.20 | loop fusion | flops 47182848 | bytes 344160 | tf_op jit(solution)/shard_map/reduce_sum | solution.py:18
  101.4 0.0 copy-start.1
  101.4 35.9 %fusion.23 = bf16[2048,1024]{1,0:T(8,128)(2,1)} fusion(bf16[3072,1024]{1,0:T(8,128)(2,1)} %bitcast.12, f32[3072,2048]{1,0:T(8,128)} %fusion.36, f32[2048]{0:T(1024)S(1)} %convert_element_type.24, f32[3072]{0:T(1024)S(1)} %bitcast.13), kind=kOutput, calls=%fused_computation.29 | convolution fusion | flops 13019119616 | bytes 35672064 | tf_op jit(solution)/shard_map/dot_general | solution.py:58
  137.3 0.0 copy-done.1
  137.3 0.0 reduce-scatter.2.cloned.1.call-update
  137.4 51.3 %reduce-scatter.2.cloned.1.call-done = bf16[256,1024]{1,0:T(8,128)(2,1)} async-done(((bf16[2048,1024]{1,0:T(8,128)(2,1)}), bf16[256,1024]{1,0:T(8,128)(2,1)}) %reduce-scatter.2.cloned.1.call-update) | async-done | bytes 524304 | tf_op jit(solution)/shard_map/reduce_scatter | solution.py:57
  188.7 44.2 %all-reduce.1 = f32[256,1024]{1,0:T(8,128)S(1)} all-reduce(bf16[256,1024]{1,0:T(8,128)(2,1)} %reduce-scatter.2.cloned.1.call-done), channel_id=1, replica_groups=mesh['grp'=4,'cand'=8] {'grp'}, use_global_device_ids=true, to_apply=%region_2.0 | all-reduce | flops 262144 | bytes 1572864 | tf_op jit(solution)/shard_map/psum | solution.py:65
  232.9 0.9 multiply_reduce_fusion
  233.8 12.4 %psum.15 = f32[]{:T(128)} all-reduce(f32[]{:T(128)} %multiply_reduce_fusion), channel_id=1, replica_groups=mesh['grp'=4,'cand'=8] {'cand'}, use_global_device_ids=true, to_apply=%region_4.0 | all-reduce | flops 1 | bytes 8 | tf_op jit(solution)/shard_map/psum | solution.py:66
  246.9 1.0 broadcast_multiply_fusion
Async XLA Ops:
  7.2 42.3 %all-gather.2.cloned.1.call-start = ((), (), s32[]{:S(2)}) async-start(), calls=%async_computation.1 | async-start | bytes 4718592 | tf_op jit(solution)/shard_map/all_gather | solution.py:34
  7.9 180.8 %reduce-scatter.2.cloned.1.call-start = ((), (), s32[]{:S(2)}) async-start(), calls=%async_computation.2 | async-start | bytes 4718592 | tf_op jit(solution)/shard_map/reduce_scatter | solution.py:57
  69.1 21.1 %copy-start = (f32[24]{0:T(128)S(1)}, f32[24]{0:T(128)}, u32[]{:S(2)}) copy-start(f32[24]{0:T(128)} %param.11) | copy-start | bytes 292
  101.4 36.0 %copy-start.1 = (f32[24,128]{1,0:T(8,128)}, f32[24,128]{1,0:T(8,128)S(1)}, u32[]{:S(2)}) copy-start(f32[24,128]{1,0:T(8,128)S(1)} %fusion.13) | copy-start | bytes 36868
Sparse Core Ops, SparseCore 0:
  9.9 39.5 all-gather.1
  137.5 51.1 reduce-scatter.1
where the time goes:
time: 255 us
  blocking collectives  86 us (34%)
  waiting for transfers between devices  70.5 us (28%)
  matrix products  67.5 us (26%)
  other arithmetic  15.2 us (6%)
  between operations  14.8 us (6%)
    reduce_scatter x1, waiting for transfers between devices, per_device(): lax.psum_scatter(lax.dot_general(grad_pre, cand_rows, (((0,), (0,)), ((),...  51.3 us
    psum x1, blocking collectives, per_device(): summed = lax.psum(owned, 'grp')  44.2 us
    dot_general x1, matrix products, per_device(): lax.dot_general(grad_pre, cand_rows, (((0,), (0,)), ((), ())), preferred_...  35.9 us
    dot_general x1, matrix products, per_device(): lax.dot_general(cand_rows, lax.all_gather(hidden_weight, 'cand', axis=0,...  19.7 us
    all_gather x1, waiting for transfers between devices, per_device(): lax.all_gather(hidden_weight, 'cand', axis=0, tiled=True)  18.5 us
    psum x1, blocking collectives, per_device(): squares = lax.psum(jnp.sum(summed * summed), 'cand')  12.4 us
    dot_general x1, matrix products, per_device(): jnp.dot(acts.astype(jnp.bfloat16), score_weight, preferred_element_type=j...  11.9 us
    reduce_sum x1, other arithmetic, pair_lambdas(): return jnp.sum(weight * toward * jax.nn.sigmoid(toward * margin), axis=-1)  11.2 us
  transfers between devices with their start and end apart: 2, of which 2 were waited for; matrix products, arithmetic and copies ran while one was open for 1% of the time, Pallas kernels for 0%

commit v1 on v0

--- a/solution.py
+++ b/solution.py
@@ -62,7 +62,7 @@
         scatter_dimension=0,
         tiled=True,
     ).astype(jnp.float32)
-    summed = lax.psum(owned, "grp")
+    summed = jnp.sum(lax.all_gather(owned, "grp"), axis=0)
     squares = lax.psum(jnp.sum(summed * summed), "cand")
     entries = summed.shape[0] * summed.shape[1] * lax.axis_size("cand")
     scale = lax.rsqrt(squares / entries + EPS)

time: 255 us -> 298 us (1.17)
  waiting for transfers between devices: 70.5 us -> 151 us
  blocking collectives: 86 us -> 43.4 us
  other arithmetic: 15.2 us -> 20.1 us
    all_gather x0 -> x1, waiting for transfers between devices: none -> 80.9 us  [per_device(): summed = jnp.sum(lax.all_gather(owned, 'grp'), axis=0)]
    psum x1 -> x0, blocking collectives: 44.2 us -> none  [per_device(): summed = lax.psum(owned, 'grp')]
  transfers between devices with their start and end apart: 2 -> 3, of which waited for: 2 -> 3; matrix products, arithmetic and copies ran while one was open for 1% -> 1% of each run, Pallas kernels for 0% -> 0%
where the time goes in v1:
time: 298 us
  waiting for transfers between devices  151 us (51%)
  matrix products  67.5 us (23%)
  blocking collectives  43.4 us (15%)
  other arithmetic  20.1 us (7%)
  between operations  14.5 us (5%)
    all_gather x1, waiting for transfers between devices, per_device(): summed = jnp.sum(lax.all_gather(owned, 'grp'), axis=0)  80.9 us
    reduce_scatter x1, waiting for transfers between devices, per_device(): lax.psum_scatter(lax.dot_general(grad_pre, cand_rows, (((0,), (0,)), ((),...  51.3 us
    dot_general x1, matrix products, per_device(): lax.dot_general(grad_pre, cand_rows, (((0,), (0,)), ((), ())), preferred_...  35.9 us
    dot_general x1, matrix products, per_device(): lax.dot_general(cand_rows, lax.all_gather(hidden_weight, 'cand', axis=0,...  19.7 us
    all_gather x1, waiting for transfers between devices, per_device(): lax.all_gather(hidden_weight, 'cand', axis=0, tiled=True)  18.5 us
    psum x1, blocking collectives, per_device(): squares = lax.psum(jnp.sum(summed * summed), 'cand')  14.1 us
    dot_general x1, matrix products, per_device(): jnp.dot(acts.astype(jnp.bfloat16), score_weight, preferred_element_type=j...  11.9 us
    reduce_sum x1, other arithmetic, pair_lambdas(): return jnp.sum(weight * toward * jax.nn.sigmoid(toward * margin), axis=-1)  11.2 us
  transfers between devices with their start and end apart: 3, of which 3 were waited for; matrix products, arithmetic and copies ran while one was open for 1% of the time, Pallas kernels for 0%

profile of v1, /device:TPU:0, one launch (start us, length us, event | category | flops | bytes accessed | tf_op | source)
XLA Modules:
  0.0 297.7 jit_solution(6015672379931126881)
XLA Ops:
  7.2 0.0 all-gather.4.cloned.1.call-start
  7.2 0.7 all-gather.4.cloned.1.call-update
  7.9 0.0 reduce-scatter.2.cloned.1.call-start
  7.9 0.7 reshape.20
  8.6 0.7 convert_element_type.22
  9.3 0.7 exponential_add_fusion
  10.0 10.7 %all_gather.21 = f32[24,1024]{1,0:T(8,128)S(1)} all-gather(f32[24,128]{1,0:T(8,128)S(1)} %exponential_add_fusion), channel_id=1, replica_groups=mesh['grp'=4,'cand'=8] {'cand'}, dimensions={1}, use_global_device_ids=true | all-gather | bytes 110592 | tf_op jit(solution)/shard_map/all_gather | solution.py:49
  20.7 0.7 multiply_divide_fusion
  21.5 9.5 %all_gather.22 = f32[24,1024]{1,0:T(8,128)S(1)} all-gather(f32[24,128]{1,0:T(8,128)S(1)} %multiply_divide_fusion), channel_id=1, replica_groups=mesh['grp'=4,'cand'=8] {'cand'}, dimensions={1}, use_global_device_ids=true | all-gather | bytes 110592 | tf_op jit(solution)/shard_map/all_gather | solution.py:50
  31.0 18.5 %all-gather.4.cloned.1.call-done = bf16[2048,1024]{1,0:T(8,128)(2,1)} async-done(((bf16[256,1024]{1,0:T(8,128)(2,1)}), bf16[2048,1024]{1,0:T(8,128)(2,1)}) %all-gather.4.cloned.1.call-update) | async-done | bytes 4194320 | tf_op jit(solution)/shard_map/all_gather | solution.py:34
  49.5 19.7 %fusion.36 = f32[3072,2048]{1,0:T(8,128)} fusion(bf16[3072,1024]{1,0:T(8,128)(2,1)} %bitcast.13, bf16[2048,1024]{1,0:T(8,128)(2,1)} %all-gather.4.cloned.1.call-done), kind=kOutput, calls=%fused_computation.44 | convolution fusion | flops 12884901888 | bytes 35651584 | tf_op jit(solution)/shard_map/dot_general | solution.py:32
  69.1 0.0 copy-start
  69.1 11.9 %fusion.20 = f32[1,3072]{1,0:T(1,128)S(1)} fusion(bf16[2048,1]{0,1:T(2,128)(2,1)S(1)} %reshape.20, f32[3072,2048]{1,0:T(8,128)} %fusion.36), kind=kOutput, calls=%fused_computation.27 | convolution fusion | flops 69206016 | bytes 25182208 | tf_op jit(solution)/shard_map/dot_general | solution.py:39
  81.1 9.1 %all_gather.24 = f32[24,1024]{1,0:T(8,128)S(1)} all-gather(f32[24,128]{1,0:T(8,128)S(1)} %bitcast.11), channel_id=1, replica_groups=mesh['grp'=4,'cand'=8] {'cand'}, dimensions={1}, use_global_device_ids=true | all-gather | bytes 110592 | tf_op jit(solution)/shard_map/all_gather | solution.py:48
  90.2 0.0 copy-done
  90.2 11.2 %fusion.13 = f32[24,128]{1,0:T(8,128)S(1)} fusion(f32[24,1024]{1,0:T(8,128)S(1)} %all_gather.24, f32[24,128]{1,0:T(8,128)S(1)} %bitcast.12, f32[24]{0:T(128)S(1)} %copy-done, f32[24,128]{1,0:T(8,128)S(1)} %multiply_divide_fusion, f32[24,1024]{1,0:T(8,128)S(1)} %all_gather.22, f32[24,128]{1,0:T(8,128)S(1)} %exponential_add_fusion, f32[24,1024]{1,0:T(8,128)S(1)} %all_gather.21), kind=kLoop, calls=%fused_computation.20 | loop fusion | flops 47182848 | bytes 344160 | tf_op jit(solution)/shard_map/reduce_sum | solution.py:18
  101.4 0.0 copy-start.1
  101.4 35.9 %fusion.23 = bf16[2048,1024]{1,0:T(8,128)(2,1)} fusion(bf16[3072,1024]{1,0:T(8,128)(2,1)} %bitcast.14, f32[3072,2048]{1,0:T(8,128)} %fusion.36, f32[2048]{0:T(1024)S(1)} %convert_element_type.22, f32[3072]{0:T(1024)S(1)} %bitcast.15), kind=kOutput, calls=%fused_computation.29 | convolution fusion | flops 13019119616 | bytes 35672064 | tf_op jit(solution)/shard_map/dot_general | solution.py:58
  137.4 0.0 copy-done.1
  137.4 0.0 reduce-scatter.2.cloned.1.call-update
  137.4 0.0 all-gather.6.cloned.1.call-start
  137.5 51.3 %reduce-scatter.2.cloned.1.call-done = bf16[256,1024]{1,0:T(8,128)(2,1)} async-done(((bf16[2048,1024]{1,0:T(8,128)(2,1)}), bf16[256,1024]{1,0:T(8,128)(2,1)}) %reduce-scatter.2.cloned.1.call-update) | async-done | bytes 524304 | tf_op jit(solution)/shard_map/reduce_scatter | solution.py:57
  188.7 2.1 all_gather.28
  190.9 0.0 all-gather.6.cloned.1.call-update
  190.9 80.9 %all-gather.6.cloned.1.call-done = f32[1024,1024]{1,0:T(8,128)} async-done(((f32[256,1024]{1,0:T(8,128)}), f32[1024,1024]{1,0:T(8,128)}) %all-gather.6.cloned.1.call-update) | async-done | bytes 4194320 | tf_op jit(solution)/shard_map/all_gather | solution.py:65
  271.8 2.7 reduce_sum.28
  274.5 0.9 multiply_reduce_fusion
  275.4 14.1 %psum.7 = f32[]{:T(128)} all-reduce(f32[]{:T(128)} %multiply_reduce_fusion), channel_id=1, replica_groups=mesh['grp'=4,'cand'=8] {'cand'}, use_global_device_ids=true, to_apply=%region_4.0 | all-reduce | flops 1 | bytes 8 | tf_op jit(solution)/shard_map/psum | solution.py:66
  290.1 1.0 broadcast_multiply_fusion
Async XLA Ops:
  7.2 42.3 %all-gather.4.cloned.1.call-start = ((), (), s32[]{:S(2)}) async-start(), calls=%async_computation.1 | async-start | bytes 4718592 | tf_op jit(solution)/shard_map/all_gather | solution.py:34
  7.9 180.8 %reduce-scatter.2.cloned.1.call-start = ((), (), s32[]{:S(2)}) async-start(), calls=%async_computation.2 | async-start | bytes 4718592 | tf_op jit(solution)/shard_map/reduce_scatter | solution.py:57
  69.1 21.1 %copy-start = (f32[24]{0:T(128)S(1)}, f32[24]{0:T(128)}, u32[]{:S(2)}) copy-start(f32[24]{0:T(128)} %param.11) | copy-start | bytes 292
  101.4 36.0 %copy-start.1 = (f32[24,128]{1,0:T(8,128)}, f32[24,128]{1,0:T(8,128)S(1)}, u32[]{:S(2)}) copy-start(f32[24,128]{1,0:T(8,128)S(1)} %fusion.13) | copy-start | bytes 36868
  137.4 134.4 %all-gather.6.cloned.1.call-start = ((), (), s32[]{:S(2)}) async-start(), calls=%async_computation.3 | async-start | bytes 5242880 | tf_op jit(solution)/shard_map/all_gather | solution.py:65
Sparse Core Ops, SparseCore 0:
  9.9 39.5 all-gather.3
  137.5 51.1 reduce-scatter.1
  191.0 80.7 all-gather.5
